TPU v7x, 32 devices: a whole 2x2x4 slice. The times are simulated.
32 devices in a mesh: seq: 4 (over y, x), rep: 8 (over z, core).
Axes of the slice: x: 2, y: 2, z: 4, core: 2. Of those that a mesh axis runs over, the one named last changes fastest.
Arguments:
- tile_embed: bfloat16 [8, 4096, 768], P('rep', 'seq'), may hold values from -6 to 6
- tile_source: int32 [8, 4096], P('rep', 'seq'), may hold values from 0 to 4095, as said below
- slide_len: int32 [8], P('rep'), may hold values from 2048 to 4096
- grad_out: bfloat16 [8, 4096, 768], P('rep', 'seq'), may hold values from -6 to 6
- w_query: bfloat16 [768, 768], replicated, may hold values from -0.11727427342914273 to 0.11727427342914273
- w_key: bfloat16 [768, 768], replicated, may hold values from -0.11727427342914273 to 0.11727427342914273
- w_value: bfloat16 [768, 768], replicated, may hold values from -0.21875 to 0.21875
- w_out: bfloat16 [768, 768], replicated, may hold values from -0.21875 to 0.21875
Outputs:
- encoded: bfloat16 [8, 4096, 768], P('rep', 'seq')
- embed_grad: bfloat16 [8, 4096, 768], P('rep', 'seq')
- grad_query: float32 [768, 768], replicated
- grad_key: float32 [768, 768], replicated
- grad_value: float32 [768, 768], replicated
- grad_outproj: float32 [768, 768], replicated
Inputs may be any that keep to these rules, and one draw needn't show every extreme that they name: For each slide, tile_source is a permutation of 0 to 4095; each run of 1024 slide positions (aligned) takes exactly 1024 // (number of such runs) rows from each aligned run of 1024 rows of tile_embed.
All inputs are finite; a program needn't handle non-finite values.
Results may differ from a plain program's by a relative error of at most 0.0025.
The roundings to bfloat16 on the way count: a program that leaves them out, or rounds other values in their place, can miss the bound.
Values may be sent and summed in bfloat16 or wider, within the bound.
No kernel may reach another device: no remote copies, remote signals or barrier semaphores. Data moves between devices by JAX's collectives and lax.ppermute only.
A program may use at most 192 MiB of HBM per device.

v0:
```python
import jax
import jax.numpy as jnp
from jax import lax
from jax.sharding import PartitionSpec as P

HEADS = 16
SEG = 1024
RATE = 16
NEGATIVE = -1e30


def chosen(dilation, head_count):
    return jnp.arange(dilation)[:, None] == (jnp.arange(head_count) % dilation)[None, :]


def sparse_rows(dense, dilation):
    row_count, head_count, trailing = dense.shape
    blocks = dense.astype(jnp.float32).reshape(
        row_count // dilation, dilation, head_count, trailing
    )
    selected = chosen(dilation, head_count)[None, :, :, None]
    return jnp.sum(jnp.where(selected, blocks, jnp.float32(0.0)), axis=1)


def spread_rows(sparse, dilation, filler):
    row_count, head_count, trailing = sparse.shape
    selected = chosen(dilation, head_count)[None, :, :, None]
    spread = jnp.where(selected, sparse[:, None], jnp.float32(filler))
    return spread.reshape(row_count * dilation, head_count, trailing)


def product(pattern, left_side, right_side):
    return jnp.einsum(pattern, left_side, right_side, preferred_element_type=jnp.float32)


def masked_scores(queries, key_rows, key_ok, pieces, scaling):
    scores = product("nqd,nkd->nqk", queries, key_rows) * scaling
    return jnp.where(key_ok.reshape(pieces, 1, -1), scores, NEGATIVE)


def head_forward(queries, key_rows, values, key_ok, pieces, scaling):
    head_width = queries.shape[-1]
    queries = queries.reshape(pieces, -1, head_width)
    key_rows = key_rows.reshape(pieces, -1, head_width)
    values = values.reshape(pieces, -1, head_width)
    scores = masked_scores(queries, key_rows, key_ok, pieces, scaling)
    maxima = jnp.max(scores, axis=-1)
    weights = jnp.exp(scores - maxima[..., None])
    totals = jnp.sum(weights, axis=-1)
    numerator = product("nqk,nkd->nqd", weights.astype(jnp.bfloat16), values)
    return (numerator.reshape(-1, head_width), maxima.reshape(-1), totals.reshape(-1))


def split_pieces(arrays, pieces):
    return tuple((member.reshape(pieces, -1, member.shape[-1]) for member in arrays))


def score_terms(queries, key_rows, values, key_ok, log_total, upstream, deltas, pieces, scaling):
    scores = masked_scores(queries, key_rows, key_ok, pieces, scaling)
    probabilities = jnp.exp(scores - log_total.reshape(pieces, -1, 1))
    prob_grad = product("nqd,nkd->nqk", upstream, values)
    score_grad = (probabilities * (prob_grad - deltas.reshape(pieces, -1, 1))).astype(jnp.bfloat16)
    return (probabilities, score_grad)


def head_backward(queries, key_rows, values, key_ok, log_total, upstream, deltas, pieces, scaling):
    head_width = queries.shape[-1]
    queries, key_rows, values, upstream = split_pieces(
        (queries, key_rows, values, upstream), pieces
    )
    probabilities, score_grad = score_terms(
        queries, key_rows, values, key_ok, log_total, upstream, deltas, pieces, scaling
    )
    value_grad = product("nqk,nqd->nkd", probabilities.astype(jnp.bfloat16), upstream)
    query_grad = product("nqk,nkd->nqd", score_grad, key_rows) * scaling
    key_grad = product("nqk,nqd->nkd", score_grad, queries) * scaling
    return (
        query_grad.reshape(-1, head_width),
        key_grad.reshape(-1, head_width),
        value_grad.reshape(-1, head_width),
    )


def heads_map(function, arrays, pieces, scaling):
    transposed = tuple((jnp.moveaxis(member, 1, 0) for member in arrays))
    results = lax.map(lambda members: function(*members, pieces, scaling), transposed)
    return tuple((jnp.moveaxis(member, 0, 1) for member in results))


def merge_parts(local_part, remote, dilation):
    numer_local, max_local, total_local = local_part
    numer_far = spread_rows(remote[0], dilation, 0.0)
    max_far = spread_rows(remote[1][..., None], dilation, NEGATIVE)[..., 0]
    total_far = spread_rows(remote[2][..., None], dilation, 0.0)[..., 0]
    highest = jnp.maximum(max_local, max_far)
    weight_local = jnp.exp(max_local - highest)
    weight_far = jnp.exp(max_far - highest)
    combined = total_local * weight_local + total_far * weight_far
    output = (numer_local * weight_local[..., None] + numer_far * weight_far[..., None]) / combined[
        ..., None
    ]
    return (output, highest + jnp.log(combined))


def project(left_side, right_side):
    return jnp.dot(left_side, right_side, preferred_element_type=jnp.float32)


def per_device(tile_embed, tile_source, slide_len, grad_out, w_query, w_key, w_value, w_out):
    owned_rows = tile_embed[0]
    source = tile_source[0]
    row_count, features = owned_rows.shape
    stripes = lax.axis_size("seq")
    stripe = lax.axis_index("seq")
    portion = row_count // stripes
    owner_dev = source // row_count
    ordering = jnp.argsort(owner_dev, stable=True)
    wanted = (source % row_count)[ordering].reshape(stripes, portion)
    requested = lax.all_to_all(wanted, "seq", split_axis=0, concat_axis=0, tiled=True)
    picked = jnp.take(owned_rows, requested.reshape(-1), axis=0).reshape(stripes, portion, features)
    arrived = lax.all_to_all(picked, "seq", split_axis=0, concat_axis=0, tiled=True).reshape(
        row_count, features
    )
    embedded = jnp.zeros_like(arrived).at[ordering].set(arrived)
    length = slide_len[0]
    upstream_in = grad_out[0]
    head_dim = features // HEADS
    scaling = head_dim ** (-0.5)
    positions = stripe * row_count + jnp.arange(row_count)
    valid_rows = positions < length
    queries = project(embedded, w_query).astype(jnp.bfloat16).reshape(row_count, HEADS, head_dim)
    key_rows = project(embedded, w_key).astype(jnp.bfloat16).reshape(row_count, HEADS, head_dim)
    values = project(embedded, w_value).astype(jnp.bfloat16).reshape(row_count, HEADS, head_dim)
    local_ok = jnp.broadcast_to(valid_rows[:, None], (row_count, HEADS))
    local_part = heads_map(
        head_forward, (queries, key_rows, values, local_ok), row_count // SEG, scaling
    )
    sparse_q = sparse_rows(queries, RATE).astype(jnp.bfloat16)
    sparse_k = sparse_rows(key_rows, RATE).astype(jnp.bfloat16)
    sparse_v = sparse_rows(values, RATE).astype(jnp.bfloat16)
    near_count = sparse_k.shape[0]
    far_k, far_v = (
        lax.all_gather(sparse_k.reshape(near_count, features), "seq", axis=0, tiled=True),
        lax.all_gather(sparse_v.reshape(near_count, features), "seq", axis=0, tiled=True),
    )
    far_count = far_k.shape[0]
    far_k = far_k.reshape(far_count, HEADS, head_dim)
    far_v = far_v.reshape(far_count, HEADS, head_dim)
    sparse_pos = jnp.arange(far_count)[:, None] * RATE + (jnp.arange(HEADS) % RATE)[None, :]
    sparse_ok = sparse_pos < length
    remote = heads_map(head_forward, (sparse_q, far_k, far_v, sparse_ok), 1, scaling)
    output, log_total = merge_parts(local_part, remote, RATE)
    attended = (
        (output * valid_rows[:, None, None]).astype(jnp.bfloat16).reshape(row_count, features)
    )
    encoded = (embedded.astype(jnp.float32) + project(attended, w_out)).astype(jnp.bfloat16)
    upstream = (
        (project(upstream_in, w_out.T) * valid_rows[:, None])
        .astype(jnp.bfloat16)
        .reshape(row_count, HEADS, head_dim)
    )
    deltas = jnp.sum(upstream.astype(jnp.float32) * output, axis=-1)
    grad_outproj = jnp.einsum(
        "td,te->de", attended, upstream_in, preferred_element_type=jnp.float32
    )
    local_grads = heads_map(
        head_backward,
        (queries, key_rows, values, local_ok, log_total, upstream, deltas),
        row_count // SEG,
        scaling,
    )
    sparse_up = sparse_rows(upstream, RATE).astype(jnp.bfloat16)
    sparse_delta = sparse_rows(deltas[..., None], RATE)[..., 0]
    sparse_total = sparse_rows(log_total[..., None], RATE)[..., 0]
    remote_grads = heads_map(
        head_backward,
        (sparse_q, far_k, far_v, sparse_ok, sparse_total, sparse_up, sparse_delta),
        1,
        scaling,
    )
    key_back, value_back = (
        lax.psum_scatter(
            remote_grads[1].reshape(far_count, features), "seq", scatter_dimension=0, tiled=True
        ),
        lax.psum_scatter(
            remote_grads[2].reshape(far_count, features), "seq", scatter_dimension=0, tiled=True
        ),
    )
    key_back = key_back.reshape(near_count, HEADS, head_dim)
    value_back = value_back.reshape(near_count, HEADS, head_dim)
    query_far = remote_grads[0]
    query_grad = (
        (local_grads[0] + spread_rows(query_far, RATE, 0.0))
        .astype(jnp.bfloat16)
        .reshape(row_count, features)
    )
    key_grad = (
        (local_grads[1] + spread_rows(key_back, RATE, 0.0))
        .astype(jnp.bfloat16)
        .reshape(row_count, features)
    )
    value_grad = (
        (local_grads[2] + spread_rows(value_back, RATE, 0.0))
        .astype(jnp.bfloat16)
        .reshape(row_count, features)
    )
    embed_grad = upstream_in.astype(jnp.float32) + project(query_grad, w_query.T)
    embed_grad = embed_grad + project(key_grad, w_key.T)
    embed_grad = (embed_grad + project(value_grad, w_value.T)).astype(jnp.bfloat16)
    grad_query = jnp.einsum("td,te->de", embedded, query_grad, preferred_element_type=jnp.float32)
    grad_key = jnp.einsum("td,te->de", embedded, key_grad, preferred_element_type=jnp.float32)
    grad_value = jnp.einsum("td,te->de", embedded, value_grad, preferred_element_type=jnp.float32)
    summed = lax.psum((grad_query, grad_key, grad_value, grad_outproj), ("seq", "rep"))
    return (encoded[None], embed_grad[None], summed[0], summed[1], summed[2], summed[3])


def solution(mesh):
    return jax.shard_map(
        per_device,
        mesh=mesh,
        in_specs=(
            P("rep", "seq", None),
            P("rep", "seq"),
            P("rep"),
            P("rep", "seq", None),
            P(),
            P(),
            P(),
            P(),
        ),
        out_specs=(P("rep", "seq", None), P("rep", "seq", None), P(), P(), P(), P()),
        check_vma=False,
    )
```

profile of v0, /device:TPU:0, one launch (start us, length us, event | category | flops | bytes accessed | tf_op | source)
XLA Modules:
  0.0 939.3 jit_solution(3229480369411910893)
XLA Ops:
  8.0 4.4 sort.17
  12.4 4.5 gather_fusion
  16.9 9.7 %all_to_all.14 = s32[4,1,256]{2,1,0:T(1,128)S(1)} all-to-all(s32[4,1,256]{2,1,0:T(1,128)S(1)} %bitcast.389), channel_id=1, replica_groups=mesh['seq'=4,'rep'=8] {'seq'}, dimensions={0} | all-to-all | bytes 8192 | tf_op jit(solution)/shard_map/all_to_all | solution.py:119
  32.0 4.5 all-to-all-start.1
  43.2 7.8 reshape.434
  53.0 4.9 copy.100
  58.0 6.4 scatter_custom_fusion
  69.7 7.8 reshape.431
  82.9 7.8 reshape.432
  90.7 4.3 convolution_convert_fusion
  98.1 7.8 reshape.433
  105.9 14.5 %select_reduce_fusion = (bf16[64,16,48]{2,1,0:T(8,128)(2,1)}, bf16[64,16,48]{2,1,0:T(8,128)(2,1)S(1)}, bf16[64,16,48]{2,1,0:T(8,128)(2,1)S(1)}, bf16[64,16,48]{2,1,0:T(8,128)(2,1)}) fusion(f32[64,16,16,48]{3,2,1,0:T(8,128)} %reshape.434, pred[16,16]{1,0:T(8,128)(4,1)S(1)} %iota_compare_fusion, f32[64,16,16,48]{3,2,1,0:T(8,128)} %reshape.432, ...), kind=kLoop, calls=%fused_computation.133 | loop fusion | flops 6094848 | bytes 12976384 | tf_op jit(solution)/shard_map/reduce_sum | solution.py:22
  120.6 10.6 %all_gather.6 = bf16[256,768]{1,0:T(8,128)(2,1)S(1)} all-gather(bf16[64,768]{1,0:T(8,128)(2,1)S(1)} %convert_element_type.144), channel_id=1, replica_groups=mesh['seq'=4,'rep'=8] {'seq'}, dimensions={0}, use_global_device_ids=true | all-gather | bytes 491520 | tf_op jit(solution)/shard_map/all_gather | solution.py:143
  132.2 8.9 all_gather.7
  143.7 26.0 %while.57 = (s32[]{:T(128)}, f32[16,64,48]{1,2,0:T(8,128)S(1)}, f32[16,64]{1,0:T(8,128)S(1)}, f32[16,64]{1,0:T(8,128)S(1)}, pred[16,256]{1,0:T(8,128)(4,1)S(1)},...) while((s32[]{:T(128)}, f32[16,64,48]{1,2,0:T(8,128)S(1)}, ...), condition=%wide.region_12.13_spmd, body=%wide.region_9.12_spmd.sunk | while | flops 3260290 | bytes 374129 | solution.py:86
  187.5 142.6 %while.56 = (s32[]{:T(128)}, f32[16,1024,48]{1,2,0:T(8,128)}, f32[16,1024]{1,0:T(8,128)S(1)}, f32[16,1024]{1,0:T(8,128)S(1)}, pred[16,1024]{1,0:T(8,128)(4,1)S(1...) while((s32[]{:T(128)}, f32[16,1024,48]{1,2,0:T(8,128)}, ...), condition=%wide.region_5.6_spmd, body=%wide.region_2.5_spmd.sunk | while | flops 212858880 | bytes 30383244 | solution.py:86
  332.5 7.9 copy.83
  340.4 13.4 %multiply_convert_fusion.1 = (bf16[1024,16,48]{2,1,0:T(8,128)(2,1)}, f32[1024,16,48]{2,1,0:T(8,128)S(1)}) fusion(f32[1024]{0:T(1024)S(1)} %copy-done.34, f32[1024,16]{1,0:T(8,128)} %copy.97, f32[1024,16]{1,0:T(8,128)S(1)} %copy.96, f32[64,16,48]{2,1,0:T(8,128)S(1)} %copy.95, pred[1024,16]{1,0:T(8,128)(4,1)S(1)} %copy-done.19, f32[1024,16]{1,0:T(8,128)S(1)} %copy.93, ...), kind=kLoop, calls=%fused_computation.135 | loop fusion | flops 5505024 | bytes 8278016 | tf_op jit(solution)/shard_map/convert_element_type | solution.py:154
  357.3 98.4 %while.59 = (s32[]{:T(128)}, f32[16,64,48]{1,2,0:T(8,128)S(1)}, f32[16,256,48]{1,2,0:T(8,128)}, f32[16,256,48]{1,2,0:T(8,128)}, pred[16,256]{1,0:T(8,128)(4,1)},...) while((s32[]{:T(128)}, f32[16,64,48]{1,2,0:T(8,128)S(1)}, ...), condition=%wide.region_20.21_spmd, body=%wide.region_19.20_spmd.sunk | while | flops 7994370 | bytes 687741 | solution.py:86
  470.3 181.2 %while.58 = (s32[]{:T(128)}, f32[16,1024,48]{1,2,0:T(8,128)}, f32[16,1024,48]{1,2,0:T(8,128)}, f32[16,1024,48]{1,2,0:T(8,128)}, pred[16,1024]{1,0:T(8,128)(4,1)S...) while((s32[]{:T(128)}, f32[16,1024,48]{1,2,0:T(8,128)}, ...), condition=%wide.region_15.16_spmd, body=%wide.region_14.15_spmd.sunk | while | flops 513900544 | bytes 21337212 | solution.py:86
  651.8 7.9 copy.102
  659.6 7.8 copy.112
  667.5 7.9 copy.115
  675.3 5.5 copy.98
  687.8 15.2 %fusion.110 = (bf16[1024,16,48]{2,1,0:T(8,128)(2,1)}, bf16[1024,16,48]{2,1,0:T(8,128)(2,1)}, bf16[1024,16,48]{2,1,0:T(8,128)(2,1)}) fusion(f32[16,1024,48]{2,0,1:T(8,128)} %copy.102, f32[64,16,48]{2,1,0:T(8,128)S(1)} %copy.110, pred[1024,16]{1,0:T(8,128)(4,1)} %copy.94, f32[64,16,48]{2,1,0:T(8,128)S(1)} %copy.113, f32[16,1024,48]{2,0,1:T(8,128)} %copy.112, ...), kind=kLoop, calls=%fused_computation.127 | loop fusion | flops 7077888 | bytes 14761984 | tf_op jit(solution)/shard_map/convert_element_type | solution.py:194
  703.0 5.5 copy.111
  712.7 5.5 copy.114
  718.2 4.2 fusion.131
  722.5 4.4 copy.117
  727.0 4.2 fusion.132
  731.2 5.0 fusion.117
  742.9 179.8 %all-reduce.3.cloned.1.call-done = (f32[768,768]{1,0:T(8,128)}, f32[768,768]{1,0:T(8,128)}, f32[768,768]{1,0:T(8,128)}, f32[768,768]{1,0:T(8,128)}) async-done(((f32[768,768]{1,0:T(8,128)}, f32[768,768]{1,0:T(8,128)}, f32[768,768]{1,0:T(8,128)}, f32[768,768]{1,0:T(8,128)}), (f32[768,768]{1,0:T(8,128)}, f32[768,768]{1,0:T(8,128)}, f32[768,768]{1,0:T(8,128)}, ...) | async-done | bytes 9437200 | tf_op jit(solution)/shard_map/psum | solution.py:213
  (612 shorter events, 543.6 us)
Async XLA Ops:
  7.2 19.4 %copy-start = (bf16[1,1024,768]{2,1,0:T(8,128)(2,1)S(1)}, bf16[1,1024,768]{2,1,0:T(8,128)(2,1)}, u32[]{:S(2)}) copy-start(bf16[1,1024,768]{2,1,0:T(8,128)(2,1)} %param.16) | copy-start | bytes 4718596
  32.0 6.3 copy-start.13
  32.0 26.0 %all-to-all-start.1 = ((bf16[4,256,768]{2,1,0:T(8,128)(2,1)}), bf16[4,256,768]{2,1,0:T(8,128)(2,1)}, u32[]{:S(2)}, u32[]{:S(2)}) async-start(bf16[4,256,768]{2,1,0:T(8,128)(2,1)} %broadcast_select_fusion), calls=%async_computation.1 | async-start | bytes 3145728 | tf_op jit(solution)/shard_map/all_to_all | solution.py:121
  36.5 648.5 %reduce-scatter.7.cloned.1.call-start = ((), (), s32[]{:S(2)}) async-start(), calls=%async_computation.4 | async-start | bytes 983040
  41.0 12.0 %copy-start.4 = (bf16[1024,768]{0,1:T(8,128)(2,1)}, bf16[1024,768]{0,1:T(8,128)(2,1)S(1)}, u32[]{:S(2)}) copy-start(bf16[1024,768]{0,1:T(8,128)(2,1)S(1)} %multiply_convert_fusion.2) | copy-start | bytes 4718596
  52.1 5.8 copy-start.26
  64.4 3.3 copy-start.15
  80.7 10.1 %copy-start.6 = (bf16[1024,768]{0,1:T(8,128)(2,1)}, bf16[1024,768]{0,1:T(8,128)(2,1)S(1)}, u32[]{:S(2)}) copy-start(bf16[1024,768]{0,1:T(8,128)(2,1)S(1)} %convolution_convert_fusion.1) | copy-start | bytes 4718596
  131.2 12.4 %copy-start.35 = (f32[16,64]{1,0:T(8,128)S(1)}, f32[16,64]{1,0:T(8,128)}, u32[]{:S(2)}) copy-start(f32[16,64]{1,0:T(8,128)} %custom-call.7) | copy-start | bytes 12292
  169.6 3.2 copy-start.9
  169.6 3.2 copy-start.22
  169.7 9.4 copy-start.30
  173.8 5.2 copy-start.7
  179.0 3.2 copy-start.8
  182.2 3.2 copy-start.36
  182.2 5.2 copy-start.28
  182.2 5.2 copy-start.29
  187.5 142.6 %copy-start.24 = (f32[1024,16]{0,1:T(8,128)S(1)}, f32[1024,16]{0,1:T(8,128)}, u32[]{:S(2)}) copy-start(f32[1024,16]{0,1:T(8,128)} %broadcast_in_dim.318) | copy-start | bytes 196612
  187.5 142.6 %copy-start.25 = (f32[1024,16]{0,1:T(8,128)S(1)}, f32[1024,16]{0,1:T(8,128)}, u32[]{:S(2)}) copy-start(f32[1024,16]{0,1:T(8,128)} %broadcast_in_dim.325) | copy-start | bytes 196612
  187.5 142.6 %copy-start.27 = (pred[1024,16]{0,1:T(8,128)(4,1)S(1)}, pred[1024,16]{0,1:T(8,128)(4,1)}, u32[]{:S(2)}) copy-start(pred[1024,16]{0,1:T(8,128)(4,1)} %copy-done.26) | copy-start | bytes 49156
  332.5 7.9 copy-start.19
  332.5 7.9 copy-start.34
  340.4 13.4 %copy-start.3 = (bf16[1024,16,48]{2,1,0:T(8,128)(2,1)S(1)}, bf16[1024,16,48]{2,1,0:T(8,128)(2,1)}, u32[]{:S(2)}) copy-start(bf16[1024,16,48]{2,1,0:T(8,128)(2,1)} %copy.100) | copy-start | bytes 4718596
  357.2 100.8 %copy-start.5 = (bf16[1024,768]{0,1:T(8,128)(2,1)S(1)}, bf16[1024,768]{0,1:T(8,128)(2,1)}, u32[]{:S(2)}) copy-start(bf16[1024,768]{0,1:T(8,128)(2,1)} %copy-done.4) | copy-start | bytes 4718596
  458.0 228.4 %reduce-scatter.9.cloned.1.call-start = ((), (), s32[]{:S(2)}) async-start(), calls=%async_computation.5 | async-start | bytes 983040
  463.7 459.1 %all-reduce.3.cloned.1.call-start = ((), (), s32[]{:S(2)}) async-start(), calls=%async_computation.6 | async-start | bytes 18874368 | tf_op jit(solution)/shard_map/psum | solution.py:213
  675.3 5.5 copy-start.14
  703.0 5.5 copy-start.16
  731.2 5.0 copy-start.17
  731.2 5.0 copy-start.37
  922.7 3.4 copy-start.12
  928.6 3.9 copy-start.1
  (26 other events, 51.9 us)
Sparse Core Ops, SparseCore 0:
  458.1 26.4 reduce-scatter.6
  488.0 26.1 reduce-scatter.8
  731.3 191.3 all-reduce.2
where the time goes:
time: 954 us; the launch traced here: 939 us
  matrix products  421 us (44%)
  local copies, waits for them, and re-layouts  215 us (23%)
  waiting for transfers between devices  180 us (19%)
  other arithmetic  71.3 us (7%)
  blocking collectives  29.2 us (3%)
  between operations  15.2 us (2%)
    dot_general x224, matrix products, product(): jnp.einsum(pattern, left_side, right_side, preferred_element_type=jnp.flo...  380 us
    psum x1, waiting for transfers between devices, per_device(): lax.psum((grad_query, grad_key, grad_value, grad_outproj), ('seq', 'rep'))  180 us
    while x9, local copies, waits for them, and re-layouts, heads_map(): lax.map(lambda members: function(*members, pieces, scaling), transposed)  34.5 us
    while x32, local copies, waits for them, and re-layouts  30.9 us
    convert_element_type x6, local copies, waits for them, and re-layouts, sparse_rows(): dense.astype(jnp.float32)  30.7 us
    dot_general x8, matrix products, project(): return jnp.dot(left_side, right_side, preferred_element_type=jnp.float32)  24 us
  transfers between devices with their start and end apart: 4, of which 1 were waited for; matrix products, arithmetic and copies ran while one was open for 27% of the time, Pallas kernels for 0%

commit v1 on v0

--- a/solution.py
+++ b/solution.py
@@ -210,7 +210,8 @@
     grad_query = jnp.einsum("td,te->de", embedded, query_grad, preferred_element_type=jnp.float32)
     grad_key = jnp.einsum("td,te->de", embedded, key_grad, preferred_element_type=jnp.float32)
     grad_value = jnp.einsum("td,te->de", embedded, value_grad, preferred_element_type=jnp.float32)
-    summed = lax.psum((grad_query, grad_key, grad_value, grad_outproj), ("seq", "rep"))
+    _list_copies = lambda in_array: lax.psum(lax.psum(in_array, "rep"), "seq")
+    summed = _list_copies((grad_query, grad_key, grad_value, grad_outproj))
     return (encoded[None], embed_grad[None], summed[0], summed[1], summed[2], summed[3])
 
 

time: 954 us -> 1150 us (1.21)
  waiting for transfers between devices: 180 us -> 377 us
    psum x1 -> x2, waiting for transfers between devices: 180 us -> 377 us  [per_device(): _list_copies = lambda in_array: lax.psum(lax.psum(in_array, 'rep'), 'seq')]
  transfers between devices with their start and end apart: 4 -> 5, of which waited for: 1 -> 2; matrix products, arithmetic and copies ran while one was open for 27% -> 23% of each run, Pallas kernels for 0% -> 0%
where the time goes in v1:
time: 1150 us; the launch traced here: 1140 us
  matrix products  421 us (37%)
  waiting for transfers between devices  377 us (33%)
  local copies, waits for them, and re-layouts  215 us (19%)
  other arithmetic  71.3 us (6%)
  blocking collectives  29.2 us (3%)
  between operations  15.2 us (1%)
    dot_general x224, matrix products, product(): jnp.einsum(pattern, left_side, right_side, preferred_element_type=jnp.flo...  380 us
    psum x2, waiting for transfers between devices, per_device(): _list_copies = lambda in_array: lax.psum(lax.psum(in_array, 'rep'), 'seq')  377 us
    while x9, local copies, waits for them, and re-layouts, heads_map(): lax.map(lambda members: function(*members, pieces, scaling), transposed)  34.5 us
    while x32, local copies, waits for them, and re-layouts  31 us
    convert_element_type x6, local copies, waits for them, and re-layouts, sparse_rows(): dense.astype(jnp.float32)  30.7 us
    dot_general x8, matrix products, project(): return jnp.dot(left_side, right_side, preferred_element_type=jnp.float32)  24 us
  transfers between devices with their start and end apart: 5, of which 2 were waited for; matrix products, arithmetic and copies ran while one was open for 23% of the time, Pallas kernels for 0%

profile of v1, /device:TPU:0, one launch (start us, length us, event | category | flops | bytes accessed | tf_op | source)
XLA Modules:
  0.0 1136.3 jit_solution(5038618839337548659)
XLA Ops:
  8.0 4.4 sort.17
  12.4 4.5 gather_fusion
  16.9 9.7 all_to_all.14
  32.0 4.5 all-to-all-start.1
  43.4 7.8 reshape.434
  53.2 4.9 copy.100
  58.1 6.4 scatter_custom_fusion
  69.9 7.8 reshape.431
  83.0 7.8 reshape.432
  90.9 4.3 convolution_convert_fusion
  98.2 7.8 reshape.433
  106.0 14.5 %select_reduce_fusion = (bf16[64,16,48]{2,1,0:T(8,128)(2,1)}, bf16[64,16,48]{2,1,0:T(8,128)(2,1)S(1)}, bf16[64,16,48]{2,1,0:T(8,128)(2,1)S(1)}, bf16[64,16,48]{2,1,0:T(8,128)(2,1)}) fusion(f32[64,16,16,48]{3,2,1,0:T(8,128)} %reshape.434, pred[16,16]{1,0:T(8,128)(4,1)S(1)} %iota_compare_fusion, f32[64,16,16,48]{3,2,1,0:T(8,128)} %reshape.432, ...), kind=kLoop, calls=%fused_computation.133 | loop fusion | flops 6094848 | bytes 12976384 | tf_op jit(solution)/shard_map/reduce_sum | solution.py:22
  120.7 10.6 all_gather.6
  132.3 8.9 all_gather.7
  143.8 26.0 %while.57 = (s32[]{:T(128)}, f32[16,64,48]{1,2,0:T(8,128)S(1)}, f32[16,64]{1,0:T(8,128)S(1)}, f32[16,64]{1,0:T(8,128)S(1)}, pred[16,256]{1,0:T(8,128)(4,1)S(1)},...) while((s32[]{:T(128)}, f32[16,64,48]{1,2,0:T(8,128)S(1)}, ...), condition=%wide.region_12.13_spmd, body=%wide.region_9.12_spmd.sunk | while | flops 3260290 | bytes 374129 | solution.py:86
  187.6 142.7 %while.56 = (s32[]{:T(128)}, f32[16,1024,48]{1,2,0:T(8,128)}, f32[16,1024]{1,0:T(8,128)S(1)}, f32[16,1024]{1,0:T(8,128)S(1)}, pred[16,1024]{1,0:T(8,128)(4,1)S(1...) while((s32[]{:T(128)}, f32[16,1024,48]{1,2,0:T(8,128)}, ...), condition=%wide.region_5.6_spmd, body=%wide.region_2.5_spmd.sunk | while | flops 212858880 | bytes 30383244 | solution.py:86
  332.8 7.9 copy.83
  340.7 13.4 %multiply_convert_fusion.1 = (bf16[1024,16,48]{2,1,0:T(8,128)(2,1)}, f32[1024,16,48]{2,1,0:T(8,128)S(1)}) fusion(f32[1024]{0:T(1024)S(1)} %copy-done.34, f32[1024,16]{1,0:T(8,128)} %copy.97, f32[1024,16]{1,0:T(8,128)S(1)} %copy.96, f32[64,16,48]{2,1,0:T(8,128)S(1)} %copy.95, pred[1024,16]{1,0:T(8,128)(4,1)S(1)} %copy-done.19, f32[1024,16]{1,0:T(8,128)S(1)} %copy.93, ...), kind=kLoop, calls=%fused_computation.135 | loop fusion | flops 5505024 | bytes 8278016 | tf_op jit(solution)/shard_map/convert_element_type | solution.py:154
  357.5 98.4 %while.59 = (s32[]{:T(128)}, f32[16,64,48]{1,2,0:T(8,128)S(1)}, f32[16,256,48]{1,2,0:T(8,128)}, f32[16,256,48]{1,2,0:T(8,128)}, pred[16,256]{1,0:T(8,128)(4,1)},...) while((s32[]{:T(128)}, f32[16,64,48]{1,2,0:T(8,128)S(1)}, ...), condition=%wide.region_20.21_spmd, body=%wide.region_19.20_spmd.sunk | while | flops 7994370 | bytes 687741 | solution.py:86
  470.6 181.2 %while.58 = (s32[]{:T(128)}, f32[16,1024,48]{1,2,0:T(8,128)}, f32[16,1024,48]{1,2,0:T(8,128)}, f32[16,1024,48]{1,2,0:T(8,128)}, pred[16,1024]{1,0:T(8,128)(4,1)S...) while((s32[]{:T(128)}, f32[16,1024,48]{1,2,0:T(8,128)}, ...), condition=%wide.region_15.16_spmd, body=%wide.region_14.15_spmd.sunk | while | flops 513900544 | bytes 21337212 | solution.py:86
  652.1 7.9 copy.102
  660.0 7.8 copy.112
  667.8 7.9 copy.115
  675.7 5.5 copy.98
  688.2 15.2 %fusion.110 = (bf16[1024,16,48]{2,1,0:T(8,128)(2,1)}, bf16[1024,16,48]{2,1,0:T(8,128)(2,1)}, bf16[1024,16,48]{2,1,0:T(8,128)(2,1)}) fusion(f32[16,1024,48]{2,0,1:T(8,128)} %copy.102, f32[64,16,48]{2,1,0:T(8,128)S(1)} %copy.110, pred[1024,16]{1,0:T(8,128)(4,1)} %copy.94, f32[64,16,48]{2,1,0:T(8,128)S(1)} %copy.113, f32[16,1024,48]{2,0,1:T(8,128)} %copy.112, ...), kind=kLoop, calls=%fused_computation.127 | loop fusion | flops 7077888 | bytes 14761984 | tf_op jit(solution)/shard_map/convert_element_type | solution.py:194
  703.4 5.5 copy.111
  713.1 5.5 copy.114
  722.8 4.4 copy.117
  727.3 4.2 fusion.132
  731.6 195.8 %all-reduce.5.cloned.1.call-done = (f32[768,768]{1,0:T(8,128)}, f32[768,768]{1,0:T(8,128)}, f32[768,768]{1,0:T(8,128)}, f32[768,768]{1,0:T(8,128)}) async-done(((f32[768,768]{1,0:T(8,128)}, f32[768,768]{1,0:T(8,128)}, f32[768,768]{1,0:T(8,128)}, f32[768,768]{1,0:T(8,128)}), (f32[768,768]{1,0:T(8,128)}, f32[768,768]{1,0:T(8,128)}, f32[768,768]{1,0:T(8,128)}, ...) | async-done | bytes 9437200 | tf_op jit(solution)/shard_map/psum | solution.py:213
  927.5 5.0 fusion.117
  938.3 181.4 %all-reduce.7.cloned.1.call-done = (f32[768,768]{1,0:T(8,128)}, f32[768,768]{1,0:T(8,128)}, f32[768,768]{1,0:T(8,128)}, f32[768,768]{1,0:T(8,128)}) async-done(((f32[768,768]{1,0:T(8,128)}, f32[768,768]{1,0:T(8,128)}, f32[768,768]{1,0:T(8,128)}, f32[768,768]{1,0:T(8,128)}), (f32[768,768]{1,0:T(8,128)}, f32[768,768]{1,0:T(8,128)}, f32[768,768]{1,0:T(8,128)}, ...) | async-done | bytes 9437200 | tf_op jit(solution)/shard_map/psum | solution.py:213
  (615 shorter events, 547.4 us)
Async XLA Ops:
  7.2 19.4 %copy-start = (bf16[1,1024,768]{2,1,0:T(8,128)(2,1)S(1)}, bf16[1,1024,768]{2,1,0:T(8,128)(2,1)}, u32[]{:S(2)}) copy-start(bf16[1,1024,768]{2,1,0:T(8,128)(2,1)} %param.16) | copy-start | bytes 4718596
  32.0 6.4 copy-start.13
  32.0 26.1 %all-to-all-start.1 = ((bf16[4,256,768]{2,1,0:T(8,128)(2,1)}), bf16[4,256,768]{2,1,0:T(8,128)(2,1)}, u32[]{:S(2)}, u32[]{:S(2)}) async-start(bf16[4,256,768]{2,1,0:T(8,128)(2,1)} %broadcast_select_fusion), calls=%async_computation.1 | async-start | bytes 3145728 | tf_op jit(solution)/shard_map/all_to_all | solution.py:121
  36.5 648.9 %reduce-scatter.7.cloned.1.call-start = ((), (), s32[]{:S(2)}) async-start(), calls=%async_computation.4 | async-start | bytes 983040
  41.1 12.0 %copy-start.4 = (bf16[1024,768]{0,1:T(8,128)(2,1)}, bf16[1024,768]{0,1:T(8,128)(2,1)S(1)}, u32[]{:S(2)}) copy-start(bf16[1024,768]{0,1:T(8,128)(2,1)S(1)} %multiply_convert_fusion.2) | copy-start | bytes 4718596
  52.3 5.8 copy-start.26
  64.5 3.3 copy-start.15
  80.8 10.0 copy-start.6
  131.4 12.4 %copy-start.35 = (f32[16,64]{1,0:T(8,128)S(1)}, f32[16,64]{1,0:T(8,128)}, u32[]{:S(2)}) copy-start(f32[16,64]{1,0:T(8,128)} %custom-call.7) | copy-start | bytes 12292
  169.8 3.2 copy-start.9
  169.8 9.4 copy-start.30
  173.9 5.2 copy-start.7
  179.2 3.2 copy-start.8
  182.4 3.2 copy-start.36
  182.4 5.3 copy-start.28
  182.4 5.3 copy-start.29
  187.6 142.7 %copy-start.24 = (f32[1024,16]{0,1:T(8,128)S(1)}, f32[1024,16]{0,1:T(8,128)}, u32[]{:S(2)}) copy-start(f32[1024,16]{0,1:T(8,128)} %broadcast_in_dim.318) | copy-start | bytes 196612
  187.6 142.7 %copy-start.25 = (f32[1024,16]{0,1:T(8,128)S(1)}, f32[1024,16]{0,1:T(8,128)}, u32[]{:S(2)}) copy-start(f32[1024,16]{0,1:T(8,128)} %broadcast_in_dim.325) | copy-start | bytes 196612
  187.6 142.7 %copy-start.27 = (pred[1024,16]{0,1:T(8,128)(4,1)S(1)}, pred[1024,16]{0,1:T(8,128)(4,1)}, u32[]{:S(2)}) copy-start(pred[1024,16]{0,1:T(8,128)(4,1)} %copy-done.26) | copy-start | bytes 49156
  332.7 7.9 copy-start.19
  332.7 7.9 copy-start.34
  340.7 13.4 %copy-start.3 = (bf16[1024,16,48]{2,1,0:T(8,128)(2,1)S(1)}, bf16[1024,16,48]{2,1,0:T(8,128)(2,1)}, u32[]{:S(2)}) copy-start(bf16[1024,16,48]{2,1,0:T(8,128)(2,1)} %copy.100) | copy-start | bytes 4718596
  357.5 100.8 %copy-start.5 = (bf16[1024,768]{0,1:T(8,128)(2,1)S(1)}, bf16[1024,768]{0,1:T(8,128)(2,1)}, u32[]{:S(2)}) copy-start(bf16[1024,768]{0,1:T(8,128)(2,1)} %copy-done.4) | copy-start | bytes 4718596
  458.2 228.5 %reduce-scatter.9.cloned.1.call-start = ((), (), s32[]{:S(2)}) async-start(), calls=%async_computation.5 | async-start | bytes 983040
  463.9 463.5 %all-reduce.5.cloned.1.call-start = ((), (), s32[]{:S(2)}) async-start(), calls=%async_computation.6 | async-start | bytes 18874368 | tf_op jit(solution)/shard_map/psum | solution.py:213
  675.7 5.5 copy-start.14
  703.3 5.5 copy-start.16
  731.6 388.2 %all-reduce.7.cloned.1.call-start = ((), (), s32[]{:S(2)}) async-start(), calls=%async_computation.7 | async-start | bytes 18874368 | tf_op jit(solution)/shard_map/psum | solution.py:213
  927.4 5.0 copy-start.17
  927.4 5.0 copy-start.37
  1119.8 3.4 copy-start.12
  1125.6 3.9 copy-start.1
  (27 other events, 54.0 us)
Sparse Core Ops, SparseCore 0:
  458.4 26.4 reduce-scatter.6
  488.3 26.1 reduce-scatter.8
  731.7 195.6 all-reduce.4
  931.2 188.5 all-reduce.6
